TPU v7x, 32 devices: a whole 2x2x4 slice. The times are simulated.
32 devices in a mesh: wide: 4 (over x, core), narrow: 8 (over z, y).
Axes of the slice: x: 2, y: 2, z: 4, core: 2. Of those that a mesh axis runs over, the one named last changes fastest.
Arguments:
- single: bfloat16 [48, 128, 768], P('narrow', 'wide'), may hold values from -6 to 6
- pair: bfloat16 [128, 128, 128], P('wide', 'narrow'), may hold values from -6 to 6
- restype: int32 [128], P('wide'), may hold values from 0 to 31
- chain: int32 [128], replicated, may hold values from 0 to 7, never falling along the last dimension, each value on 1 to 32 neighbouring positions
- residue_type_embedding: float32 [32, 768], replicated, may hold values from -6 to 6
- pair_bias_weight: bfloat16 [2, 16, 128], replicated, may hold values from -41 to 41, as said below
- shared_chain_score: float32 [2, 16], replicated, may hold values from -8 to 8
- query_weight: bfloat16 [2, 768, 768], replicated, may hold values from -0.21875 to 0.21875
- key_weight: bfloat16 [2, 768, 768], replicated, may hold values from -0.21875 to 0.21875
- value_weight: bfloat16 [2, 768, 768], replicated, may hold values from -0.21875 to 0.21875
- output_weight: bfloat16 [2, 768, 768], replicated, may hold values from -0.21875 to 0.21875
Outputs:
- updated: bfloat16 [48, 128, 768], P('narrow', 'wide')
Inputs may be any that keep to these rules, and one draw needn't show every extreme that they name: `pair_bias_weight`: each entry is a real number.
All inputs are finite; a program needn't handle non-finite values.
Results may differ from a plain program's by a relative error of at most 0.0084.
Values may be sent and summed in bfloat16 or wider, within the bound.
No kernel may reach another device: no remote copies, remote signals or barrier semaphores. Data moves between devices by JAX's collectives and lax.ppermute only.
A program may use at most 128 MiB of HBM per device.

v0:
```python
import math
import jax
import jax.numpy as jnp
from jax import lax
from jax.sharding import PartitionSpec as P

epsilon_norm = 1e-05


def normalize(inputs):
    average = jnp.mean(inputs, axis=-1, keepdims=True)
    centered = inputs - average
    spread_squared = jnp.mean(centered * centered, axis=-1, keepdims=True)
    return centered * lax.rsqrt(spread_squared + epsilon_norm)


def attend(stacked, layer_head_bias, score_scale):
    head_dim = stacked.shape[-1] // 3
    queries = stacked[..., :head_dim]
    key_rows = stacked[..., head_dim : 2 * head_dim]
    value_rows = stacked[..., 2 * head_dim :]
    batch_count, row_count, head_count, _ = queries.shape
    running_max = jnp.full((batch_count, head_count, row_count), -jnp.inf, jnp.float32)
    running_sum = jnp.zeros((batch_count, head_count, row_count), jnp.float32)
    running_out = jnp.zeros((batch_count, row_count, head_count, head_dim), jnp.float32)
    key_piece = lax.all_gather(key_rows, "wide", axis=1, tiled=True)
    value_piece = lax.all_gather(value_rows, "wide", axis=1, tiled=True)
    scores = (
        jnp.einsum("aqhd,akhd->ahqk", queries, key_piece, preferred_element_type=jnp.float32)
        * score_scale
        + layer_head_bias[None]
    )
    refreshed_peak = jnp.max(scores, axis=-1)
    rescale = jnp.exp(running_max - refreshed_peak)
    weights_exp = jnp.exp(scores - refreshed_peak[..., None])
    running_sum = running_sum * rescale + jnp.sum(weights_exp, axis=-1)
    contrib = jnp.einsum(
        "ahqk,akhd->aqhd",
        weights_exp.astype(jnp.bfloat16),
        value_piece,
        preferred_element_type=jnp.float32,
    )
    running_out = running_out * jnp.swapaxes(rescale, 1, 2)[..., None] + contrib
    return (running_out / jnp.swapaxes(running_sum, 1, 2)[..., None]).astype(jnp.bfloat16)


def shards(
    single,
    pair,
    restype,
    chain,
    residue_type_embedding,
    pair_bias_weight,
    shared_chain_score,
    query_weight,
    key_weight,
    value_weight,
    output_weight,
):
    sample_count, row_count, model_width = single.shape
    head_count = pair_bias_weight.shape[1]
    head_dim = model_width // head_count
    block_count = query_weight.shape[0]
    row_begin = lax.axis_index("wide") * row_count
    onehot = (
        restype[:, None] == jnp.arange(residue_type_embedding.shape[0], dtype=jnp.int32)[None, :]
    ).astype(jnp.float32)
    embedded = jnp.dot(onehot, residue_type_embedding, precision=lax.Precision.HIGHEST)
    residual = single.astype(jnp.float32) + embedded[None]
    pair_norm = normalize(pair.astype(jnp.float32)).astype(jnp.bfloat16)
    bias_panel = jnp.einsum(
        "ijc,bhc->hbij", pair_norm, pair_bias_weight, preferred_element_type=jnp.float32
    )
    row_chain = lax.dynamic_slice_in_dim(chain, row_begin, row_count)
    same_strand_indicator = (row_chain[:, None] == chain[None, :]).astype(jnp.float32)
    complete_bias = lax.all_gather(bias_panel, "narrow", axis=3, tiled=True)
    score_scale = 1.0 / math.sqrt(head_dim)
    for present_segment_index in range(block_count):
        layer_head_bias = (
            complete_bias[:, present_segment_index]
            + shared_chain_score[present_segment_index][:, None, None] * same_strand_indicator[None]
        )
        normed = (
            normalize(residual).astype(jnp.bfloat16).reshape(sample_count * row_count, model_width)
        )
        query_part = jnp.dot(
            normed, query_weight[present_segment_index], preferred_element_type=jnp.float32
        ).astype(jnp.bfloat16)
        key_part = jnp.dot(
            normed, key_weight[present_segment_index], preferred_element_type=jnp.float32
        ).astype(jnp.bfloat16)
        value_part = jnp.dot(
            normed, value_weight[present_segment_index], preferred_element_type=jnp.float32
        ).astype(jnp.bfloat16)
        stacked = jnp.concatenate(
            [
                query_part.reshape(sample_count, row_count, head_count, head_dim),
                key_part.reshape(sample_count, row_count, head_count, head_dim),
                value_part.reshape(sample_count, row_count, head_count, head_dim),
            ],
            axis=-1,
        )
        regrouped = attend(stacked, layer_head_bias, score_scale)
        projected = jnp.dot(
            regrouped.reshape(sample_count * row_count, model_width),
            output_weight[present_segment_index],
            preferred_element_type=jnp.float32,
        )
        residual = residual + projected.reshape(sample_count, row_count, model_width)
    return residual.astype(jnp.bfloat16)


def solution(mesh):
    return jax.shard_map(
        shards,
        mesh=mesh,
        in_specs=(
            P("narrow", "wide", None),
            P("wide", "narrow", None),
            P("wide"),
            P(),
            P(),
            P(),
            P(),
            P(),
            P(),
            P(),
            P(),
        ),
        out_specs=P("narrow", "wide", None),
        check_vma=False,
    )
```

profile of v0, /device:TPU:0, one launch (start us, length us, event | category | flops | bytes accessed | tf_op | source)
XLA Modules:
  0.0 206.9 jit_solution(3401385552301880186)
XLA Ops:
  9.4 1.2 multiply_reduce_fusion.1
  11.7 1.7 convolution_convert_fusion.4
  15.5 1.7 convolution_convert_fusion.3
  20.2 86.1 %all_gather.16 = f32[16,2,32,128]{0,3,1,2:T(8,128)} all-gather(f32[16,2,32,16]{0,3,1,2:T(8,128)S(1)} %convolution_bitcast_fusion), channel_id=1, replica_groups=mesh['wide'=4,'narrow'=8] {'narrow'}, dimensions={3}, use_global_device_ids=true | all-gather | bytes 589824 | tf_op jit(solution)/shard_map/all_gather | solution.py:76
  106.4 3.6 %fusion = (f32[16,32,128]{0,2,1:T(8,128)S(1)}, f32[16,32,128]{0,2,1:T(8,128)}) fusion(f32[16,2,32,128]{0,3,1,2:T(8,128)} %all_gather.16, f32[16]{0:T(128)S(1)} %get-tuple-element.7, f32[32,128]{1,0:T(8,128)S(1)} %compare_convert_fusion, f32[16]{0:T(128)S(1)} %get-tuple-element.8), kind=kLoop, calls=%fused_computation.1 | loop fusion | flops 262144 | bytes 1065088 | tf_op jit(solution)/shard_map/add | solution.py:80
  110.0 2.2 %copy.24 = f32[16,32,128]{2,1,0:T(8,128)S(1)} copy(f32[16,32,128]{0,2,1:T(8,128)} %get-tuple-element.6) | data formatting | bytes 524288 | tf_op jit(solution)/shard_map/add | solution.py:80
  112.2 2.4 %convolution_convert_fusion.5 = bf16[192,768]{1,0:T(8,128)(2,1)} fusion(bf16[192,768]{1,0:T(8,128)(2,1)S(1)} %bitcast.100, bf16[2,768,768]{2,1,0:T(8,128)(2,1)} %param.18), kind=kOutput, calls=%fused_computation.27 | convolution fusion | flops 226639872 | bytes 1769472 | tf_op jit(solution)/shard_map/dot_general | solution.py:86
  114.6 1.8 reshape.119
  116.5 3.7 %fusion.46 = (f32[6,16,32]{2,1,0:T(8,128)S(1)}, f32[6,16,32,128]{3,2,1,0:T(8,128)S(1)}) fusion(f32[16,32,128]{2,1,0:T(8,128)S(1)} %copy.24, bf16[6,128,16,48]{3,1,2,0:T(8,128)(2,1)} %all-gather.5.cloned.1.call-done, bf16[6,32,16,48]{3,2,1,0:T(8,128)(2,1)S(1)} %reshape.119), kind=kOutput, calls=%fused_computation.81 | convolution fusion | flops 38925312 | bytes 3321856 | tf_op jit(solution)/shard_map/aqhd,akhd->ahqk/dot_general | solution.py:29
  122.4 4.2 %fusion.5 = bf16[6,32,16,48]{3,1,2,0:T(8,128)(2,1)S(1)} fusion(bf16[6,128,16,48]{3,1,2,0:T(8,128)(2,1)} %all-gather.7.cloned.1.call-done, f32[6,16,32,128]{3,2,1,0:T(8,128)} %copy-done.1, f32[6,32,16]{1,2,0:T(8,128)S(1)} %bitcast_add_fusion.3, f32[6,16,32]{2,1,0:T(8,128)S(1)} %get-tuple-element.9, f32[6,32,16]{1,2,0:T(8,128)S(1)} %multiply_bitcast_fusion.1), kind=kOutput, calls=%fused_computation.9 | convolution fusion | flops 38977536 | bytes 3084288 | tf_op jit(solution)/shard_map/ahqk,akhd->aqhd/dot_general | solution.py:37
  126.9 1.5 dot_general.53
  128.4 2.0 fusion.47
  131.9 2.7 %reshape.124 = bf16[6,32,16,48]{3,2,1,0:T(8,128)(2,1)} reshape(bf16[192,768]{1,0:T(8,128)(2,1)} %convolution_convert_fusion.1) | data formatting | bytes 589824 | tf_op jit(solution)/shard_map/reshape | solution.py:98
  134.6 2.2 %copy.27 = bf16[6,32,16,48]{3,1,2,0:T(8,128)(2,1)} copy(bf16[6,32,16,48]{3,2,1,0:T(8,128)(2,1)} %reshape.124) | data formatting | bytes 589824 | tf_op jit(solution)/shard_map/reshape | solution.py:98
  137.1 2.4 %convolution_convert_fusion = bf16[192,768]{1,0:T(8,128)(2,1)} fusion(bf16[192,768]{1,0:T(8,128)(2,1)S(1)} %bitcast.96, bf16[2,768,768]{2,1,0:T(8,128)(2,1)} %param.20), kind=kOutput, calls=%fused_computation.22 | convolution fusion | flops 226639872 | bytes 1769472 | tf_op jit(solution)/shard_map/dot_general | solution.py:92
  139.5 2.7 %reshape.125 = bf16[6,32,16,48]{3,2,1,0:T(8,128)(2,1)} reshape(bf16[192,768]{1,0:T(8,128)(2,1)} %convolution_convert_fusion) | data formatting | bytes 589824 | tf_op jit(solution)/shard_map/reshape | solution.py:99
  142.2 2.3 %copy.30 = bf16[6,32,16,48]{3,1,2,0:T(8,128)(2,1)} copy(bf16[6,32,16,48]{3,2,1,0:T(8,128)(2,1)} %reshape.125) | data formatting | bytes 589824 | tf_op jit(solution)/shard_map/reshape | solution.py:99
  145.2 1.7 convolution_convert_fusion.2
  146.8 1.9 reshape.123
  148.7 15.4 %all-gather.9.cloned.1.call-done = bf16[6,128,16,48]{3,1,2,0:T(8,128)(2,1)} async-done(((bf16[6,32,16,48]{3,1,2,0:T(8,128)(2,1)}), bf16[6,128,16,48]{3,1,2,0:T(8,128)(2,1)}) %all-gather.9.cloned.1.call-update) | async-done | bytes 1179664 | tf_op jit(solution)/shard_map/all_gather | solution.py:26
  164.1 4.0 %fusion.48 = (f32[6,16,32]{2,1,0:T(8,128)S(1)}, f32[6,16,32,128]{3,2,1,0:T(8,128)S(1)}) fusion(f32[16,32,128]{2,1,0:T(8,128)S(1)} %copy.29, bf16[6,128,16,48]{3,1,2,0:T(8,128)(2,1)} %all-gather.9.cloned.1.call-done, bf16[6,32,16,48]{3,2,1,0:T(8,128)(2,1)} %reshape.123), kind=kOutput, calls=%fused_computation.83 | convolution fusion | flops 38925312 | bytes 3321856 | tf_op jit(solution)/shard_map/aqhd,akhd->ahqk/dot_general | solution.py:29
  169.1 25.0 %all-gather.11.cloned.1.call-done = bf16[6,128,16,48]{3,1,2,0:T(8,128)(2,1)} async-done(((bf16[6,32,16,48]{3,1,2,0:T(8,128)(2,1)}), bf16[6,128,16,48]{3,1,2,0:T(8,128)(2,1)}) %all-gather.11.cloned.1.call-update) | async-done | bytes 1179664 | tf_op jit(solution)/shard_map/all_gather | solution.py:27
  194.1 2.8 %fusion.3 = bf16[6,32,16,48]{3,1,2,0:T(8,128)(2,1)S(1)} fusion(bf16[6,128,16,48]{3,1,2,0:T(8,128)(2,1)} %all-gather.11.cloned.1.call-done, f32[6,16,32,128]{3,2,1,0:T(8,128)S(1)} %get-tuple-element.14, f32[6,32,16]{1,2,0:T(8,128)S(1)} %bitcast_add_fusion.2, f32[6,16,32]{2,1,0:T(8,128)S(1)} %get-tuple-element.13, f32[6,32,16]{1,2,0:T(8,128)S(1)} %multiply_bitcast_fusion), kind=kOutput, calls=%fused_computation.6 | convolution fusion | flops 38977536 | bytes 3084288 | tf_op jit(solution)/shard_map/ahqk,akhd->aqhd/dot_general | solution.py:37
  198.0 2.4 %fusion.10 = bf16[6,32,768]{2,1,0:T(8,128)(2,1)} fusion(f32[6,32,768]{2,1,0:T(8,128)S(1)} %get-tuple-element.12, bf16[6,32,768]{2,1,0:T(8,128)(2,1)S(1)} %dot_general.60, bf16[2,768,768]{2,1,0:T(8,128)(2,1)} %param.21), kind=kOutput, calls=%fused_computation.21 | convolution fusion | flops 226787328 | bytes 2359296 | tf_op jit(solution)/shard_map/dot_general | solution.py:104
  (58 shorter events, 15.9 us)
Async XLA Ops:
  6.5 0.9 copy-start
  6.5 109.9 %all-gather.5.cloned.1.call-start = ((), (), s32[]{:S(2)}) async-start(), calls=%async_computation | async-start | bytes 3932160 | tf_op jit(solution)/shard_map/all_gather | solution.py:26
  15.5 106.9 %all-gather.7.cloned.1.call-start = ((), (), s32[]{:S(2)}) async-start(), calls=%async_computation.1 | async-start | bytes 3932160 | tf_op jit(solution)/shard_map/all_gather | solution.py:27
  17.2 2.2 %copy-start.3 = (bf16[32,16,128]{2,1,0:T(8,128)(2,1)S(1)}, bf16[32,16,128]{2,1,0:T(8,128)(2,1)}, u32[]{:S(2)}) copy-start(bf16[32,16,128]{2,1,0:T(8,128)(2,1)} %param.12) | copy-start | bytes 393220
  18.2 1.7 copy-start.4
  19.3 144.8 %all-gather.9.cloned.1.call-start = ((), (), s32[]{:S(2)}) async-start(), calls=%async_computation.2 | async-start | bytes 3932160 | tf_op jit(solution)/shard_map/all_gather | solution.py:26
  20.1 86.1 %copy-start.6 = (s32[128]{0:T(128)S(1)}, s32[128]{0:T(128)}, u32[]{:S(2)}) copy-start(s32[128]{0:T(128)} %param.14) | copy-start | bytes 1540
  20.1 86.3 %copy-start.5 = (f32[2,16]{1,0:T(2,128)S(1)}, f32[2,16]{1,0:T(2,128)}, u32[]{:S(2)}) copy-start(f32[2,16]{1,0:T(2,128)} %param.17) | copy-start | bytes 388
  120.2 1.2 copy-start.1
  126.5 1.8 copy-start.2
  128.4 2.4 %copy-start.7 = (bf16[2,768,768]{2,1,0:T(8,128)(2,1)S(1)}, bf16[2,768,768]{2,1,0:T(8,128)(2,1)}, u32[]{:S(2)}) copy-start(bf16[2,768,768]{2,1,0:T(8,128)(2,1)} %param.19) | copy-start | bytes 7077892
  136.8 57.2 %all-gather.11.cloned.1.call-start = ((), (), s32[]{:S(2)}) async-start(), calls=%async_computation.3 | async-start | bytes 3932160 | tf_op jit(solution)/shard_map/all_gather | solution.py:27
Sparse Core Ops, SparseCore 0:
  15.6 31.2 all-gather.4
  48.4 28.4 all-gather.6
  137.0 27.1 all-gather.8
  165.5 28.4 all-gather.10
where the time goes:
time: 208 us; the launch traced here: 207 us
  blocking collectives  86.1 us (41%)
  waiting for transfers between devices  40.5 us (19%)
  matrix products  31.2 us (15%)
  local copies, waits for them, and re-layouts  25.6 us (12%)
  between operations  13.5 us (6%)
  other arithmetic  9.64 us (5%)
    all_gather x1, blocking collectives, shards(): complete_bias = lax.all_gather(bias_panel, 'narrow', axis=3, tiled=True)  86.1 us
    all_gather x2, waiting for transfers between devices, attend(): value_piece = lax.all_gather(value_rows, 'wide', axis=1, tiled=True)  25 us
    all_gather x2, waiting for transfers between devices, attend(): key_piece = lax.all_gather(key_rows, 'wide', axis=1, tiled=True)  15.4 us
    dot_general x2, matrix products, attend(): jnp.einsum('aqhd,akhd->ahqk', queries, key_piece, preferred_element_type=...  7.66 us
    reshape x4, local copies, waits for them, and re-layouts, shards(): value_part.reshape(sample_count, row_count, head_count, head_dim)  7.09 us
    dot_general x2, matrix products, attend(): jnp.einsum('ahqk,akhd->aqhd', weights_exp.astype(jnp.bfloat16), value_pie...  6.99 us
    reshape x4, local copies, waits for them, and re-layouts, shards(): key_part.reshape(sample_count, row_count, head_count, head_dim)  6.98 us
    dot_general x2, matrix products, shards(): jnp.dot(regrouped.reshape(sample_count * row_count, model_width), output_...  4.39 us
  transfers between devices with their start and end apart: 4, of which 2 were waited for; matrix products, arithmetic and copies ran while one was open for 17% of the time, Pallas kernels for 0%

commit v1 on v0

--- a/solution.py
+++ b/solution.py
@@ -23,8 +23,11 @@
     running_max = jnp.full((batch_count, head_count, row_count), -jnp.inf, jnp.float32)
     running_sum = jnp.zeros((batch_count, head_count, row_count), jnp.float32)
     running_out = jnp.zeros((batch_count, row_count, head_count, head_dim), jnp.float32)
-    key_piece = lax.all_gather(key_rows, "wide", axis=1, tiled=True)
-    value_piece = lax.all_gather(value_rows, "wide", axis=1, tiled=True)
+    key_piece, value_piece = jnp.split(
+        lax.all_gather(jnp.concatenate([key_rows, value_rows], axis=0), "wide", axis=1, tiled=True),
+        [key_rows.shape[0]],
+        axis=0,
+    )
     scores = (
         jnp.einsum("aqhd,akhd->ahqk", queries, key_piece, preferred_element_type=jnp.float32)
         * score_scale

time: 208 us -> 208 us (level)
  matrix products: 31.2 us -> 26.9 us
  local copies, waits for them, and re-layouts: 25.6 us -> 29.3 us
  waiting for transfers between devices: 40.5 us -> 43 us
    split x0 -> x2, local copies, waits for them, and re-layouts: none -> 7.9 us  [attend(): jnp.split(lax.all_gather(jnp.concatenate([key_rows, value_rows], axis=0),...]
    dot_general x2, matrix products: 7.66 us -> 3.64 us  [attend(): jnp.einsum('aqhd,akhd->ahqk', queries, key_piece, preferred_element_type=...]
    reshape x4 -> x2, local copies, waits for them, and re-layouts: 7.09 us -> 3.67 us  [shards(): value_part.reshape(sample_count, row_count, head_count, head_dim)]
    concatenate x0 -> x2, local copies, waits for them, and re-layouts: none -> 3.3 us  [attend(): jnp.concatenate([key_rows, value_rows], axis=0)]
    reshape x4 -> x2, local copies, waits for them, and re-layouts: 6.98 us -> 3.7 us  [shards(): key_part.reshape(sample_count, row_count, head_count, head_dim)]
    all_gather x4 -> x2, waiting for transfers between devices: 40.4 us -> 42.9 us  [attend(): lax.all_gather(jnp.concatenate([key_rows, value_rows], axis=0), 'wide', a...]
  transfers between devices with their start and end apart: 4 -> 2, of which waited for: 2 -> 1; matrix products, arithmetic and copies ran while one was open for 17% -> 6% of each run, Pallas kernels for 0% -> 0%
where the time goes in v1:
time: 208 us
  blocking collectives  84.8 us (41%)
  waiting for transfers between devices  43 us (21%)
  local copies, waits for them, and re-layouts  29.3 us (14%)
  matrix products  26.9 us (13%)
  between operations  13.7 us (7%)
  other arithmetic  9.9 us (5%)
    all_gather x1, blocking collectives, shards(): complete_bias = lax.all_gather(bias_panel, 'narrow', axis=3, tiled=True)  84.8 us
    all_gather x2, waiting for transfers between devices, attend(): lax.all_gather(jnp.concatenate([key_rows, value_rows], axis=0), 'wide', a...  42.9 us
    dot_general x2, matrix products, attend(): jnp.einsum('ahqk,akhd->aqhd', weights_exp.astype(jnp.bfloat16), value_pie...  8.05 us
    split x2, local copies, waits for them, and re-layouts, attend(): jnp.split(lax.all_gather(jnp.concatenate([key_rows, value_rows], axis=0),...  7.9 us
    dot_general x2, matrix products, shards(): jnp.dot(regrouped.reshape(sample_count * row_count, model_width), output_...  4.39 us
  transfers between devices with their start and end apart: 2, of which 1 were waited for; matrix products, arithmetic and copies ran while one was open for 6% of the time, Pallas kernels for 0%

profile of v1, /device:TPU:0, one launch (start us, length us, event | category | flops | bytes accessed | tf_op | source)
XLA Modules:
  0.0 207.6 jit_solution(5615732368874308891)
XLA Ops:
  9.4 1.2 multiply_reduce_fusion.1
  11.7 1.7 convolution_convert_fusion.3
  14.4 1.7 convolution_convert_fusion.4
  17.3 1.7 copy.48
  20.8 84.8 %all_gather.10 = f32[16,2,32,128]{0,3,1,2:T(8,128)S(1)} all-gather(f32[16,2,32,16]{0,3,1,2:T(8,128)S(1)} %convolution_bitcast_fusion), channel_id=1, replica_groups=mesh['wide'=4,'narrow'=8] {'narrow'}, dimensions={3}, use_global_device_ids=true | all-gather | bytes 589824 | tf_op jit(solution)/shard_map/all_gather | solution.py:79
  105.6 1.8 fusion.8
  107.4 2.2 %copy.37 = f32[16,32,128]{2,1,0:T(8,128)S(1)} copy(f32[16,32,128]{0,2,1:T(8,128)} %get-tuple-element.10) | data formatting | bytes 524288 | tf_op jit(solution)/shard_map/add | solution.py:83
  109.6 2.4 %convolution_convert_fusion.5 = bf16[192,768]{1,0:T(8,128)(2,1)} fusion(bf16[192,768]{1,0:T(8,128)(2,1)S(1)} %bitcast.96, bf16[2,768,768]{2,1,0:T(8,128)(2,1)} %param.18), kind=kOutput, calls=%fused_computation.37 | convolution fusion | flops 226639872 | bytes 1769472 | tf_op jit(solution)/shard_map/dot_general | solution.py:89
  112.0 1.8 reshape.119
  113.9 4.0 %fusion.63 = (bf16[6,128,16,48]{3,2,0,1:T(8,128)(2,1)S(1)}, bf16[6,128,16,48]{3,2,0,1:T(8,128)(2,1)S(1)}) fusion(bf16[12,128,16,48]{3,2,0,1:T(8,128)(2,1)} %all-gather.3.cloned.1.call-done), kind=kLoop, calls=%fused_computation.92 | loop fusion | bytes 4718592 | tf_op jit(solution)/shard_map/split | solution.py:26
  117.8 1.8 fusion.64
  120.6 4.1 %fusion.13 = bf16[6,32,16,48]{3,1,2,0:T(8,128)(2,1)S(1)} fusion(bf16[6,128,16,48]{3,2,0,1:T(8,128)(2,1)S(1)} %get-tuple-element.8, f32[6,16,32,128]{3,2,1,0:T(8,128)S(1)} %get-tuple-element.14, f32[6,32,16]{1,2,0:T(8,128)S(1)} %bitcast_add_fusion.3, f32[6,16,32]{2,1,0:T(8,128)S(1)} %get-tuple-element.13, f32[6,32,16]{1,2,0:T(8,128)S(1)} %multiply_bitcast_fusion.1), kind=kOutput, calls=%fused_computation.19 | convolution fusion | flops 38977536 | bytes 3084288 | tf_op jit(solution)/shard_map/ahqk,akhd->aqhd/dot_general | solution.py:40
  125.1 1.5 dot_general.53
  126.6 2.0 fusion.65
  131.7 2.7 %reshape.125 = bf16[6,32,16,48]{3,2,1,0:T(8,128)(2,1)} reshape(bf16[192,768]{1,0:T(8,128)(2,1)} %convolution_convert_fusion) | data formatting | bytes 589824 | tf_op jit(solution)/shard_map/reshape | solution.py:102
  134.4 2.8 %reshape.124 = bf16[6,32,16,48]{3,2,1,0:T(8,128)(2,1)} reshape(bf16[192,768]{1,0:T(8,128)(2,1)} %convolution_convert_fusion.1) | data formatting | bytes 589824 | tf_op jit(solution)/shard_map/reshape | solution.py:101
  137.2 1.7 pad_maximum_fusion.1
  138.9 1.6 copy.49
  141.1 1.7 convolution_convert_fusion.2
  143.7 42.9 %all-gather.5.cloned.1.call-done = bf16[12,128,16,48]{3,2,0,1:T(8,128)(2,1)} async-done(((bf16[12,32,16,48]{3,2,0,1:T(8,128)(2,1)}), bf16[12,128,16,48]{3,2,0,1:T(8,128)(2,1)}) %all-gather.5.cloned.1.call-update) | async-done | bytes 2359312 | tf_op jit(solution)/shard_map/all_gather | solution.py:27
  186.6 3.9 %fusion.62 = (bf16[6,128,16,48]{3,2,0,1:T(8,128)(2,1)S(1)}, bf16[6,128,16,48]{3,2,0,1:T(8,128)(2,1)S(1)}) fusion(bf16[12,128,16,48]{3,2,0,1:T(8,128)(2,1)} %all-gather.5.cloned.1.call-done), kind=kLoop, calls=%fused_computation.91 | loop fusion | bytes 4718592 | tf_op jit(solution)/shard_map/split | solution.py:26
  190.6 1.8 fusion.66
  193.4 3.9 %fusion.11 = bf16[6,32,16,48]{3,1,2,0:T(8,128)(2,1)S(1)} fusion(bf16[6,128,16,48]{3,2,0,1:T(8,128)(2,1)S(1)} %get-tuple-element.6, f32[6,16,32,128]{3,2,1,0:T(8,128)S(1)} %get-tuple-element.18, f32[6,32,16]{1,2,0:T(8,128)S(1)} %bitcast_add_fusion.2, f32[6,16,32]{2,1,0:T(8,128)S(1)} %get-tuple-element.17, f32[6,32,16]{1,2,0:T(8,128)S(1)} %multiply_bitcast_fusion), kind=kOutput, calls=%fused_computation.16 | convolution fusion | flops 38977536 | bytes 3084288 | tf_op jit(solution)/shard_map/ahqk,akhd->aqhd/dot_general | solution.py:40
  198.4 2.4 %fusion.26 = bf16[6,32,768]{2,1,0:T(8,128)(2,1)} fusion(f32[6,32,768]{2,1,0:T(8,128)S(1)} %get-tuple-element.16, bf16[6,32,768]{2,1,0:T(8,128)(2,1)S(1)} %dot_general.60, bf16[2,768,768]{2,1,0:T(8,128)(2,1)} %param.21), kind=kOutput, calls=%fused_computation.31 | convolution fusion | flops 226787328 | bytes 2359296 | tf_op jit(solution)/shard_map/dot_general | solution.py:107
  (54 shorter events, 15.8 us)
Async XLA Ops:
  6.5 0.9 copy-start
  6.5 107.3 %all-gather.3.cloned.1.call-start = ((), (), s32[]{:S(2)}) async-start(), calls=%async_computation | async-start | bytes 7864320 | tf_op jit(solution)/shard_map/all_gather | solution.py:27
  19.0 0.7 copy-start.5
  19.0 0.9 copy-start.2
  19.0 1.3 copy-start.4
  19.0 1.4 copy-start.3
  19.0 167.6 %all-gather.5.cloned.1.call-start = ((), (), s32[]{:S(2)}) async-start(), calls=%async_computation.1 | async-start | bytes 7864320 | tf_op jit(solution)/shard_map/all_gather | solution.py:27
  124.8 1.8 copy-start.1
  126.6 2.4 %copy-start.6 = (bf16[2,768,768]{2,1,0:T(8,128)(2,1)S(1)}, bf16[2,768,768]{2,1,0:T(8,128)(2,1)}, u32[]{:S(2)}) copy-start(bf16[2,768,768]{2,1,0:T(8,128)(2,1)} %param.20) | copy-start | bytes 7077892
  128.8 1.8 copy-start.7
Sparse Core Ops, SparseCore 0:
  19.1 49.0 all-gather.2
  140.6 45.9 all-gather.4
